TPU v7x, 32 devices: a whole 2x2x4 slice. The times are simulated.
32 devices in a mesh: attn: 4 (over y, x), expert: 8 (over z, core).
Axes of the slice: x: 2, y: 2, z: 4, core: 2. Of those that a mesh axis runs over, the one named last changes fastest.
Arguments:
- tokens: bfloat16 [1024, 2880], P(('attn', 'expert')), may hold values from -6 to 6
- expert_ids: int32 [1024, 4], P(('attn', 'expert')), may hold values from 0 to 7, all different within a row; in each aligned block of 32 rows (0 to 31, 32 to 63, ...) at most 32 rows name the same one
- gate_probs: float32 [1024, 4], P(('attn', 'expert')), may hold values from 0.05 to 0.6
- shed_blocks: int32 [8], replicated, may hold values from 0 to 4, as said below
- partner: int32 [8], replicated, may hold values from 0 to 7, as said below
- gate_weight: bfloat16 [8, 2880, 2880], P('expert', None, 'attn'), may hold values from -0.109375 to 0.109375
- up_weight: bfloat16 [8, 2880, 2880], P('expert', None, 'attn'), may hold values from -0.109375 to 0.109375
- down_weight: bfloat16 [8, 2880, 2880], P('expert', 'attn'), may hold values from -0.109375 to 0.109375
Outputs:
- moe_out: bfloat16 [1024, 2880], P(('attn', 'expert'))
Inputs may be any that keep to these rules, and one draw needn't show every extreme that they name: `expert_ids`: in the rows of one device, no expert is named by more than 32 rows; the 4 experts of a token differ. `shed_blocks`: some expert has exactly 4. partner pairs the experts: partner[partner[e]] = e and partner[e] != e.
All inputs are finite; a program needn't handle non-finite values.
Results may differ from a plain program's by a relative error of at most 0.0081.
Values may be sent and summed in bfloat16 or wider, within the bound.
A program may use at most 128 MiB of HBM per device.

v0:
```python
import jax
import jax.numpy as jnp
from jax import lax
from jax.sharding import PartitionSpec as P

SHED_MOST = 4
SWISH_SCALE = 1.702


def lookup(table, indices):
    places = jnp.arange(table.shape[0], dtype=jnp.int32)
    return jnp.sum(jnp.where(indices[:, None] == places[None, :], table[None, :], 0), axis=1)


def row_weights(all_ids, all_probs, shed_blocks, partner, capacity, block_size):
    me = lax.axis_index("expert").astype(jnp.int32)
    named = all_ids == me
    mask = jnp.any(named, axis=1).astype(jnp.int32)
    rank = jnp.cumsum(mask) - mask
    other = lookup(partner, me[None])
    bound = (
        capacity
        - block_size * lookup(shed_blocks, other)
        + block_size * lookup(shed_blocks, me[None])
    )
    weight = jnp.sum(jnp.where(named, all_probs, 0.0), axis=1)
    return jnp.where(rank < bound, weight, 0.0)


def on_device(
    tokens, expert_ids, gate_probs, shed_blocks, partner, gate_weight, up_weight, down_weight
):
    tok_rows, model_width = tokens.shape
    top_count = expert_ids.shape[1]
    capacity = tok_rows * top_count * lax.axis_size("attn")
    block_size = capacity // 8
    both = ("attn", "expert")
    all_ids = lax.all_gather(expert_ids, both, axis=0, tiled=True)
    all_probs = lax.all_gather(gate_probs, both, axis=0, tiled=True)
    rows = lax.all_gather(tokens, both, axis=0, tiled=True)
    weight = row_weights(all_ids, all_probs, shed_blocks, partner, capacity, block_size)
    gate_part = jnp.dot(rows, gate_weight[0], preferred_element_type=jnp.float32)
    up_part = jnp.dot(rows, up_weight[0], preferred_element_type=jnp.float32)
    hidden = gate_part * jax.nn.sigmoid(SWISH_SCALE * gate_part) * (up_part + 1.0)
    hidden = (hidden * weight[:, None]).astype(jnp.bfloat16)
    share = jnp.dot(hidden, down_weight[0], preferred_element_type=jnp.float32).astype(jnp.bfloat16)
    share = lax.psum_scatter(share, "attn", scatter_dimension=0, tiled=True)
    return lax.psum_scatter(share, "expert", scatter_dimension=0, tiled=True)


def solution(mesh):
    in_specs = (
        P(("attn", "expert"), None),
        P(("attn", "expert"), None),
        P(("attn", "expert"), None),
        P(),
        P(),
        P("expert", None, "attn"),
        P("expert", None, "attn"),
        P("expert", "attn", None),
    )
    out_specs = P(("attn", "expert"), None)
    return jax.shard_map(
        on_device, mesh=mesh, in_specs=in_specs, out_specs=out_specs, check_vma=False
    )
```

profile of v0, /device:TPU:0, one launch (start us, length us, event | category | flops | bytes accessed | tf_op | source)
XLA Modules:
  0.0 226.7 jit_solution(15309892988968563415)
XLA Ops:
  6.5 0.0 all-gather.4.cloned.1.call-start
  6.5 0.7 all-gather.4.cloned.1.call-update
  7.3 0.0 reduce-scatter.5.cloned.1.call-start
  7.3 44.1 %all-gather = s32[32,32,4]{1,2,0:T(4,128)S(1)} all-gather(s32[1,32,4]{1,2,0:T(4,128)} %bitcast.24), channel_id=1, replica_groups=mesh['attn'=4,'expert'=8] {'attn','expert'}, dimensions={0}, use_global_device_ids=true | all-gather | bytes 16896 | tf_op jit(solution)/shard_map/all_gather | solution.py:38
  51.4 0.1 fusion.19
  51.4 0.1 reshape.58
  51.5 0.1 reshape.68
  51.6 1.3 fusion.14
  52.9 2.0 fusion.15
  56.1 0.3 reduce-window.9
  56.4 0.1 slice.7
  56.5 37.9 %all-gather.1 = f32[32,32,4]{1,2,0:T(4,128)S(1)} all-gather(f32[1,32,4]{1,2,0:T(4,128)} %bitcast.25), channel_id=1, replica_groups=mesh['attn'=4,'expert'=8] {'attn','expert'}, dimensions={0}, use_global_device_ids=true | all-gather | bytes 16896 | tf_op jit(solution)/shard_map/all_gather | solution.py:39
  94.4 0.1 select_reduce_fusion
  94.5 0.1 reshape.70
  94.6 0.1 slice_reduce_fusion
  94.7 0.1 fusion.13
  94.8 0.0 all-gather.4.cloned.1.call-done
  94.8 8.1 %fusion.1 = f32[1024,720]{0,1:T(8,128)S(1)} fusion(bf16[1024,2880]{1,0:T(8,128)(2,1)} %all-gather.4.cloned.1.call-done, bf16[1,2880,720]{1,2,0:T(8,128)(2,1)} %param.14), kind=kOutput, calls=%fused_computation.2 | convolution fusion | flops 4246732800 | bytes 12994560 | tf_op jit(solution)/shard_map/dot_general | solution.py:43
  102.9 16.3 %convolution_convert_fusion = bf16[1024,2880]{0,1:T(8,128)(2,1)} fusion(bf16[1,720,2880]{2,1,0:T(8,128)(2,1)} %param.15, f32[1024,720]{0,1:T(8,128)S(1)} %fusion.1, bf16[1024,2880]{1,0:T(8,128)(2,1)} %all-gather.4.cloned.1.call-done, bf16[1,2880,720]{1,2,0:T(8,128)(2,1)} %param.13, f32[1024]{0:T(1024)S(1)} %fusion.13), kind=kOutput, calls=%fused_computation | convolution fusion | flops 8503050240 | bytes 23044096 | tf_op jit(solution)/shard_map/dot_general | solution.py:46
  119.1 0.0 reduce-scatter.5.cloned.1.call-update
  119.2 0.0 reduce-scatter.7.cloned.1.call-start
  119.2 64.1 %reduce-scatter.5.cloned.1.call-done = bf16[256,2880]{0,1:T(8,128)(2,1)} async-done(((bf16[1024,2880]{0,1:T(8,128)(2,1)}), bf16[256,2880]{0,1:T(8,128)(2,1)}) %reduce-scatter.5.cloned.1.call-update) | async-done | bytes 1474576 | tf_op jit(solution)/shard_map/reduce_scatter | solution.py:47
  183.3 2.6 %copy.12 = bf16[256,2880]{1,0:T(8,128)(2,1)} copy(bf16[256,2880]{0,1:T(8,128)(2,1)} %reduce-scatter.5.cloned.1.call-done) | data formatting | bytes 2949120
  185.9 0.0 reduce-scatter.7.cloned.1.call-update
  185.9 34.3 %reduce-scatter.7.cloned.1.call-done = bf16[32,2880]{1,0:T(8,128)(2,1)} async-done(((bf16[256,2880]{1,0:T(8,128)(2,1)}), bf16[32,2880]{1,0:T(8,128)(2,1)}) %reduce-scatter.7.cloned.1.call-update) | async-done | bytes 184336 | tf_op jit(solution)/shard_map/reduce_scatter | solution.py:48
  (2 shorter events, 0.0 us)
Async XLA Ops:
  6.5 88.2 %all-gather.4.cloned.1.call-start = ((), (), s32[]{:S(2)}) async-start(), calls=%async_computation.2 | async-start | bytes 6217728 | tf_op jit(solution)/shard_map/all_gather | solution.py:40
  7.3 176.0 %reduce-scatter.5.cloned.1.call-start = ((), (), s32[]{:S(2)}) async-start(), calls=%async_computation.3 | async-start | bytes 7372800 | tf_op jit(solution)/shard_map/reduce_scatter | solution.py:47
  119.2 101.0 %reduce-scatter.7.cloned.1.call-start = ((), (), s32[]{:S(2)}) async-start(), calls=%async_computation.4 | async-start | bytes 1695744 | tf_op jit(solution)/shard_map/reduce_scatter | solution.py:48
Sparse Core Ops, SparseCore 0:
  10.2 70.8 all-gather.3
  119.3 63.9 reduce-scatter.4
  186.0 34.1 reduce-scatter.6
where the time goes:
time: 227 us
  waiting for transfers between devices  99.1 us (44%)
  blocking collectives  82 us (36%)
  matrix products  24.4 us (11%)
  between operations  14.4 us (6%)
  other arithmetic  3.78 us (2%)
  local copies, waits for them, and re-layouts  2.97 us (1%)
    reduce_scatter x1, waiting for transfers between devices, on_device(): share = lax.psum_scatter(share, 'attn', scatter_dimension=0, tiled=True)  64.1 us
    all_gather x1, blocking collectives, on_device(): all_ids = lax.all_gather(expert_ids, both, axis=0, tiled=True)  44.1 us
    all_gather x1, blocking collectives, on_device(): all_probs = lax.all_gather(gate_probs, both, axis=0, tiled=True)  37.9 us
    reduce_scatter x1, waiting for transfers between devices, on_device(): return lax.psum_scatter(share, 'expert', scatter_dimension=0, tiled=True)  34.3 us
    dot_general x1, matrix products, on_device(): jnp.dot(hidden, down_weight[0], preferred_element_type=jnp.float32)  16.3 us
    dot_general x1, matrix products, on_device(): up_part = jnp.dot(rows, up_weight[0], preferred_element_type=jnp.float32)  8.09 us
  transfers between devices with their start and end apart: 3, of which 2 were waited for; matrix products, arithmetic and copies ran while one was open for 2% of the time, Pallas kernels for 0%

commit v1 on v0

--- a/solution.py
+++ b/solution.py
@@ -35,8 +35,11 @@
     capacity = tok_rows * top_count * lax.axis_size("attn")
     block_size = capacity // 8
     both = ("attn", "expert")
-    all_ids = lax.all_gather(expert_ids, both, axis=0, tiled=True)
-    all_probs = lax.all_gather(gate_probs, both, axis=0, tiled=True)
+    all_ids, all_probs = jnp.split(
+        lax.all_gather(jnp.concatenate([expert_ids, gate_probs], axis=1), both, axis=0, tiled=True),
+        [expert_ids.shape[1]],
+        axis=1,
+    )
     rows = lax.all_gather(tokens, both, axis=0, tiled=True)
     weight = row_weights(all_ids, all_probs, shed_blocks, partner, capacity, block_size)
     gate_part = jnp.dot(rows, gate_weight[0], preferred_element_type=jnp.float32)

time: 227 us -> 215 us (0.947)
  blocking collectives: 82 us -> 44 us
  waiting for transfers between devices: 99.1 us -> 124 us
    all_gather x2 -> x1, blocking collectives: 82 us -> 44 us  [on_device(): lax.all_gather(jnp.concatenate([expert_ids, gate_probs], axis=1), both, a...]
    all_gather x1, waiting for transfers between devices: 0.01 us -> 23.5 us  [on_device(): rows = lax.all_gather(tokens, both, axis=0, tiled=True)]
  transfers between devices with their start and end apart: 3 -> 3, of which waited for: 2 -> 3; matrix products, arithmetic and copies ran while one was open for 2% -> 3% of each run, Pallas kernels for 0% -> 0%
where the time goes in v1:
time: 215 us
  waiting for transfers between devices  124 us (58%)
  blocking collectives  44 us (20%)
  matrix products  24.4 us (11%)
  between operations  14.4 us (7%)
  other arithmetic  5.07 us (2%)
  local copies, waits for them, and re-layouts  2.89 us (1%)
    reduce_scatter x1, waiting for transfers between devices, on_device(): share = lax.psum_scatter(share, 'attn', scatter_dimension=0, tiled=True)  65.6 us
    all_gather x1, blocking collectives, on_device(): lax.all_gather(jnp.concatenate([expert_ids, gate_probs], axis=1), both, a...  44 us
    reduce_scatter x1, waiting for transfers between devices, on_device(): return lax.psum_scatter(share, 'expert', scatter_dimension=0, tiled=True)  34.3 us
    all_gather x1, waiting for transfers between devices, on_device(): rows = lax.all_gather(tokens, both, axis=0, tiled=True)  23.5 us
    dot_general x1, matrix products, on_device(): jnp.dot(hidden, down_weight[0], preferred_element_type=jnp.float32)  16.3 us
    dot_general x1, matrix products, on_device(): up_part = jnp.dot(rows, up_weight[0], preferred_element_type=jnp.float32)  8.09 us
  transfers between devices with their start and end apart: 3, of which 3 were waited for; matrix products, arithmetic and copies ran while one was open for 3% of the time, Pallas kernels for 0%

profile of v1, /device:TPU:0, one launch (start us, length us, event | category | flops | bytes accessed | tf_op | source)
XLA Modules:
  0.0 214.8 jit_solution(14172072868669368088)
XLA Ops:
  6.5 0.0 all-gather.3.cloned.1.call-start
  6.5 0.7 all-gather.3.cloned.1.call-update
  7.3 0.0 reduce-scatter.5.cloned.1.call-start
  7.3 1.3 fusion.15
  8.6 2.0 fusion.16
  11.8 0.7 convert_element_type.25
  12.5 0.7 maximum_bitcast_fusion
  13.2 44.0 %all-gather = f32[32,32,8]{1,2,0:T(8,128)S(1)} all-gather(f32[1,32,8]{1,2,0:T(8,128)S(1)} %maximum_bitcast_fusion), channel_id=1, replica_groups=mesh['attn'=4,'expert'=8] {'attn','expert'}, dimensions={0}, use_global_device_ids=true | all-gather | bytes 33792 | tf_op jit(solution)/shard_map/all_gather | solution.py:39
  57.2 0.1 reshape.60
  57.4 0.3 reduce-window.9
  57.6 0.1 slice.7
  57.7 0.1 slice_reduce_fusion
  57.9 0.1 fusion.14
  58.0 23.5 %all-gather.3.cloned.1.call-done = bf16[1024,2880]{1,0:T(8,128)(2,1)} async-done(((bf16[32,2880]{1,0:T(8,128)(2,1)}), bf16[1024,2880]{1,0:T(8,128)(2,1)}) %all-gather.3.cloned.1.call-update) | async-done | bytes 5898256 | tf_op jit(solution)/shard_map/all_gather | solution.py:43
  81.4 8.1 %fusion.1 = f32[1024,720]{0,1:T(8,128)S(1)} fusion(bf16[1024,2880]{1,0:T(8,128)(2,1)} %all-gather.3.cloned.1.call-done, bf16[1,2880,720]{1,2,0:T(8,128)(2,1)} %param.14), kind=kOutput, calls=%fused_computation.2 | convolution fusion | flops 4246732800 | bytes 12994560 | tf_op jit(solution)/shard_map/dot_general | solution.py:46
  89.5 16.3 %convolution_convert_fusion = bf16[1024,2880]{0,1:T(8,128)(2,1)} fusion(bf16[1,720,2880]{2,1,0:T(8,128)(2,1)} %param.15, f32[1024,720]{0,1:T(8,128)S(1)} %fusion.1, bf16[1024,2880]{1,0:T(8,128)(2,1)} %all-gather.3.cloned.1.call-done, bf16[1,2880,720]{1,2,0:T(8,128)(2,1)} %param.13, f32[1024]{0:T(1024)S(1)} %fusion.14), kind=kOutput, calls=%fused_computation | convolution fusion | flops 8503050240 | bytes 23044096 | tf_op jit(solution)/shard_map/dot_general | solution.py:49
  105.8 0.0 reduce-scatter.5.cloned.1.call-update
  105.8 0.0 reduce-scatter.7.cloned.1.call-start
  105.9 65.6 %reduce-scatter.5.cloned.1.call-done = bf16[256,2880]{0,1:T(8,128)(2,1)} async-done(((bf16[1024,2880]{0,1:T(8,128)(2,1)}), bf16[256,2880]{0,1:T(8,128)(2,1)}) %reduce-scatter.5.cloned.1.call-update) | async-done | bytes 1474576 | tf_op jit(solution)/shard_map/reduce_scatter | solution.py:50
  171.4 2.6 %copy.14 = bf16[256,2880]{1,0:T(8,128)(2,1)} copy(bf16[256,2880]{0,1:T(8,128)(2,1)} %reduce-scatter.5.cloned.1.call-done) | data formatting | bytes 2949120
  174.0 0.0 reduce-scatter.7.cloned.1.call-update
  174.0 34.3 %reduce-scatter.7.cloned.1.call-done = bf16[32,2880]{1,0:T(8,128)(2,1)} async-done(((bf16[256,2880]{1,0:T(8,128)(2,1)}), bf16[32,2880]{1,0:T(8,128)(2,1)}) %reduce-scatter.7.cloned.1.call-update) | async-done | bytes 184336 | tf_op jit(solution)/shard_map/reduce_scatter | solution.py:51
  (5 shorter events, 0.1 us)
Async XLA Ops:
  6.5 74.9 %all-gather.3.cloned.1.call-start = ((), (), s32[]{:S(2)}) async-start(), calls=%async_computation.2 | async-start | bytes 6217728 | tf_op jit(solution)/shard_map/all_gather | solution.py:43
  7.3 164.2 %reduce-scatter.5.cloned.1.call-start = ((), (), s32[]{:S(2)}) async-start(), calls=%async_computation.3 | async-start | bytes 7372800 | tf_op jit(solution)/shard_map/reduce_scatter | solution.py:50
  105.8 102.5 %reduce-scatter.7.cloned.1.call-start = ((), (), s32[]{:S(2)}) async-start(), calls=%async_computation.4 | async-start | bytes 1695744 | tf_op jit(solution)/shard_map/reduce_scatter | solution.py:51
Sparse Core Ops, SparseCore 0:
  10.2 71.2 all-gather.2
  106.0 65.4 reduce-scatter.4
  174.2 34.1 reduce-scatter.6
